TPU v7x, 32 devices: a whole 2x2x4 slice. The times are simulated.
32 devices in a mesh: groups: 2 (over y), ep: 16 (over z, x, core), node: 1.
Axes of the slice: x: 2, y: 2, z: 4, core: 2. Of those that a mesh axis runs over, the one named last changes fastest.
Arguments:
- queries: bfloat16 [4096, 64, 576], P(('groups', 'ep'), 'node'), parts along dimension 0, may hold values from -16 to 16
- latent_kv: bfloat16 [4096, 576], P(('groups', 'ep')), parts along dimension 0, may hold values from -4 to 4
- w_value: bfloat16 [64, 512, 128], P('node'), may hold values from -0.25 to 0.25
- moe_tokens: bfloat16 [1024, 4096], P(('groups', 'ep')), parts along dimension 0, may hold values from -6 to 6
- routes: int32 [1024, 8], P(('groups', 'ep')), parts along dimension 0, may hold values from 0 to 15, all different within a row; in each aligned block of 32 rows (0 to 31, 32 to 63, ...) at most 24 rows name the same one
- router: bfloat16 [4096, 16], replicated, may hold values from -0.25 to 0.25
- w_gate: bfloat16 [16, 4096, 2048], P('ep', None, 'node'), may hold values from -0.09375 to 0.09375
- w_up: bfloat16 [16, 4096, 2048], P('ep', None, 'node'), may hold values from -0.09375 to 0.09375
- w_down: bfloat16 [16, 2048, 4096], P('ep', 'node'), may hold values from -0.125 to 0.125
Outputs:
- attention_out: bfloat16 [4096, 8192], P(('groups', 'ep'), 'node'), parts along dimension 0
- moe_out: bfloat16 [1024, 4096], P(('groups', 'ep'), 'node'), parts along dimension 0
There are 2 independent parts, one for each index of `groups`. A program takes and returns all parts, laid end to end along the dimension named above; an argument that names none is the same for every part. Nothing has to cross between parts.
Inputs may be any that keep to these rules, and one draw needn't show every extreme that they name: `routes`: each row names 8 different experts; among the 32 rows of one index of ep no expert is named by more than 24 rows, a bound that some block reaches of them.
All inputs are finite; a program needn't handle non-finite values.
Results may differ from a plain program's by a relative error of at most 0.015.
Values may be sent and summed in bfloat16 or wider, within the bound.
A program may use at most 192 MiB of HBM per device.

v0:
```python
import functools

import jax
import jax.numpy as jnp
from jax import lax
from jax.experimental import pallas as pl
from jax.experimental.pallas import tpu as pltpu
from jax.sharding import PartitionSpec as P

ROUTED_SCALE = 2.5
NEGATIVE = -1e30
LOG2E = 1.4426950408889634


def attend_kernel(per_sub, scale, me_ref, q_ref, kv_ref, wv_ref, *rest):
    out_ref = rest[-1]
    heads, seq_dev, width = q_ref.shape
    keys = kv_ref.shape[0]
    latent_width, value_width = wv_ref.shape[1], wv_ref.shape[2]
    first = me_ref[0] * seq_dev
    rows = per_sub * seq_dev
    for sub in range(heads // per_sub):
        q = q_ref[sub * per_sub : (sub + 1) * per_sub].reshape(rows, width)
        scores = lax.dot_general(
            q, kv_ref[...], (((1,), (1,)), ((), ())), preferred_element_type=jnp.float32
        )
        row = lax.broadcasted_iota(jnp.int32, (rows, keys), 0)
        col = lax.broadcasted_iota(jnp.int32, (rows, keys), 1)
        scores = jnp.where(col <= lax.rem(row, seq_dev) + first, scores, NEGATIVE)
        row_max = jnp.max(scores, axis=1, keepdims=True)
        raised = jnp.exp2((scores - row_max) * (scale * LOG2E))
        totals = jnp.sum(raised, axis=1, keepdims=True)
        context = jnp.dot(
            raised.astype(jnp.bfloat16),
            kv_ref[:, :latent_width],
            preferred_element_type=jnp.float32,
        )
        context = (context / totals).astype(jnp.bfloat16)
        for h in range(per_sub):
            head = sub * per_sub + h
            out_ref[:, head * value_width : (head + 1) * value_width] = jnp.dot(
                context[h * seq_dev : (h + 1) * seq_dev],
                wv_ref[head],
                preferred_element_type=jnp.float32,
            ).astype(out_ref.dtype)


def attend(me, q, kv, w_value, start, count, scale, prior):
    heads, seq_dev, width = q.shape
    _, latent_width, value_width = w_value.shape
    keys = kv.shape[0]
    block = min(8, count)
    per_sub = 2 if block % 2 == 0 else 1
    offset = start // block
    in_specs = [
        pl.BlockSpec(memory_space=pltpu.SMEM),
        pl.BlockSpec((block, seq_dev, width), lambda i: (i + offset, 0, 0)),
        pl.BlockSpec((keys, width), lambda i: (0, 0)),
        pl.BlockSpec((block, latent_width, value_width), lambda i: (i + offset, 0, 0)),
    ]
    args = [me, q, kv, w_value]
    aliases = {}
    if prior is not None:
        in_specs.append(pl.BlockSpec(memory_space=pl.ANY))
        args.append(prior)
        aliases = {4: 0}
    return pl.pallas_call(
        functools.partial(attend_kernel, per_sub, scale),
        grid=(count // block,),
        in_specs=in_specs,
        out_specs=pl.BlockSpec((seq_dev, block * value_width), lambda i: (0, i + offset)),
        out_shape=jax.ShapeDtypeStruct((seq_dev, heads * value_width), jnp.bfloat16),
        input_output_aliases=aliases,
        compiler_params=pltpu.CompilerParams(vmem_limit_bytes=56 * 1024 * 1024),
        cost_estimate=pl.CostEstimate(
            flops=2 * count * seq_dev * keys * (width + latent_width),
            bytes_accessed=2 * count * (seq_dev * width + latent_width * value_width),
            transcendentals=count * seq_dev * keys,
        ),
    )(*args)


def per_device(queries, latent_kv, w_value, moe_tokens, routes, router, w_gate, w_up, w_down):
    seq_dev, heads_dev, width = queries.shape
    latent_width, value_width = w_value.shape[1], w_value.shape[2]
    scale = (value_width + width - latent_width) ** (-0.5)
    me = lax.axis_index("ep")
    me_array = jnp.full((1,), me, jnp.int32)
    tokens_dev, top = routes.shape
    local_experts = w_gate.shape[0]
    ep_size = lax.axis_size("ep")
    experts = local_experts * ep_size
    model = moe_tokens.shape[1]
    tokens = tokens_dev * ep_size
    capacity = min(tokens_dev, 3 * tokens_dev * top // (2 * experts))
    slots = capacity * ep_size

    kv = lax.all_gather(latent_kv, "ep", axis=0, tiled=True)
    q = jnp.transpose(queries, (1, 0, 2))

    logits = jnp.dot(moe_tokens, router, preferred_element_type=jnp.float32)
    affinity = jax.nn.sigmoid(logits)
    named = jnp.any(routes[:, :, None] == lax.iota(jnp.int32, experts)[None, None, :], axis=1)
    kept = jnp.where(named, affinity, 0.0)
    gates = ROUTED_SCALE * kept / jnp.sum(kept, axis=1, keepdims=True)
    gate_high = gates.astype(jnp.bfloat16)
    gate_low = (gates - gate_high.astype(jnp.float32)).astype(jnp.bfloat16)
    extra = jnp.concatenate([gate_high, gate_low, named.astype(jnp.bfloat16)], axis=1)
    extra = jnp.pad(extra, ((0, 0), (0, -extra.shape[1] % 128)))
    outgoing = jnp.concatenate([moe_tokens, extra], axis=1)
    kv, outgoing, q = lax.optimization_barrier((kv, outgoing, q))
    packed = lax.all_gather(outgoing, "ep", axis=0, tiled=True)

    half = heads_dev // 2
    attention_out = attend(me_array, q, kv, w_value, 0, half, scale, None)

    packed, attention_out = lax.optimization_barrier((packed, attention_out))
    all_tokens = packed[:, :model]
    extras = packed[:, model:].astype(jnp.float32)
    contributions = jnp.zeros((tokens, model), jnp.float32)
    lower = (lax.iota(jnp.int32, tokens)[:, None] > lax.iota(jnp.int32, tokens)[None, :])
    for j in range(local_experts):
        mine = (lax.iota(jnp.int32, experts) == me * local_experts + j).astype(jnp.float32)
        pick = lambda k: jnp.sum(extras[:, k * experts : (k + 1) * experts] * mine, axis=1)
        gate_of = pick(0) + pick(1)
        member = pick(2)
        rank = jnp.dot(
            lower.astype(jnp.bfloat16),
            member.astype(jnp.bfloat16)[:, None],
            preferred_element_type=jnp.float32,
        )[:, 0].astype(jnp.int32)
        slot = jnp.where(member > 0, rank, -1)
        chosen = (slot[None, :] == lax.iota(jnp.int32, slots)[:, None]).astype(jnp.bfloat16)
        rows = jnp.dot(chosen, all_tokens, preferred_element_type=jnp.float32).astype(jnp.bfloat16)
        gate = jnp.dot(rows, w_gate[j], preferred_element_type=jnp.float32)
        upward = jnp.dot(rows, w_up[j], preferred_element_type=jnp.float32)
        hidden = (jax.nn.silu(gate) * upward).astype(jnp.bfloat16)
        partial_value = jnp.dot(hidden, w_down[j], preferred_element_type=jnp.float32)
        spread = lax.dot_general(
            chosen,
            partial_value.astype(jnp.bfloat16),
            (((0,), (0,)), ((), ())),
            preferred_element_type=jnp.float32,
        )
        contributions = contributions + gate_of[:, None] * spread
    contributions = contributions.astype(jnp.bfloat16)
    moe_out = lax.psum_scatter(contributions, "ep", scatter_dimension=0, tiled=True)
    if lax.axis_size("node") > 1:
        moe_out = lax.psum_scatter(moe_out, "node", scatter_dimension=1, tiled=True)

    contributions, attention_out = lax.optimization_barrier((contributions, attention_out))
    attention_out = attend(
        me_array, q, kv, w_value, half, heads_dev - half, scale, attention_out
    )
    return (attention_out, moe_out)


def solution(mesh):
    placed = (
        P(("groups", "ep"), "node", None),
        P(("groups", "ep"), None),
        P("node", None, None),
        P(("groups", "ep"), None),
        P(("groups", "ep"), None),
        P(),
        P("ep", None, "node"),
        P("ep", None, "node"),
        P("ep", "node", None),
    )
    return jax.shard_map(
        per_device,
        mesh=mesh,
        in_specs=placed,
        out_specs=(P(("groups", "ep"), "node"), P(("groups", "ep"), "node")),
        check_vma=False,
    )
```

profile of v0, /device:TPU:0, one launch (start us, length us, event | category | flops | bytes accessed | tf_op | source)
XLA Modules:
  0.0 236.0 jit_solution(10023523407280128540)
XLA Ops:
  7.2 0.0 all-gather.3.cloned.1.call-start
  7.2 1.7 copy.16
  9.0 0.0 all-gather.3.cloned.1.call-update
  9.0 0.0 all-gather.5.cloned.1.call-start
  9.0 0.7 fusion.27
  9.8 1.2 fusion.30
  11.0 0.1 copy.19
  11.1 14.1 %copy.18 = bf16[128,64,576]{2,0,1:T(8,128)(2,1)} copy(bf16[128,64,576]{0,2,1:T(8,128)(2,1)} %param.9) | data formatting | bytes 18874368 | tf_op args[0]
  25.1 0.7 fusion.23
  25.9 30.8 %all-gather.3.cloned.1.call-done.kv_ref = bf16[2048,576]{1,0:T(8,128)(2,1)} async-done(((bf16[128,576]{1,0:T(8,128)(2,1)}), bf16[2048,576]{1,0:T(8,128)(2,1)}) %all-gather.3.cloned.1.call-update) | async-done | bytes 2359312 | tf_op jit(solution)/shard_map/all_gather | solution.py:98
  56.7 0.0 reduce-scatter.2.cloned.1.call-start
  56.8 36.8 %shard_map.104.rest_0_ = bf16[128,8192]{1,0:T(8,128)(2,1)} custom-call(s32[1]{0:T(128)} %bitcast.me_ref, bf16[64,128,576]{2,1,0:T(8,128)(2,1)} %bitcast.24, bf16[2048,576]{1,0:T(8,128)(2,1)} %all-gather.3.cloned.1.call-done.kv_ref, bf16[64,512,128]{2,1,0:T(8,128)(2,1)} %wv_ref.3), custom_call_target="tpu_custom_call" | custom-call | flops 18253611008 | bytes 8912896 | tf_op jit(solution)/shard_map/pallas_call | solution.py:67
  93.6 15.5 %all-gather.5.cloned.1.call-done = bf16[512,4224]{1,0:T(8,128)(2,1)} async-done(((bf16[32,4224]{1,0:T(8,128)(2,1)}), bf16[512,4224]{1,0:T(8,128)(2,1)}) %all-gather.5.cloned.1.call-update) | async-done | bytes 4325392 | tf_op jit(solution)/shard_map/all_gather | solution.py:112
  109.1 0.9 slice_convert_fusion
  110.0 0.4 fusion.25
  110.5 0.2 fusion.19
  110.7 4.0 %convolution_convert_fusion = bf16[384,4096]{1,0:T(8,128)(2,1)S(1)} fusion(bf16[512,4224]{1,0:T(8,128)(2,1)} %all-gather.5.cloned.1.call-done, s32[512]{0:T(512)S(1)} %convert_select_fusion), kind=kOutput, calls=%fused_computation.8 | convolution fusion | flops 1612382208 | bytes 7342080 | tf_op jit(solution)/shard_map/dot_general | solution.py:134
  114.8 1.6 copy-done.3
  116.4 12.0 %fusion.4 = f32[384,2048]{1,0:T(8,128)} fusion(bf16[384,4096]{1,0:T(8,128)(2,1)S(1)} %convolution_convert_fusion, bf16[1,4096,2048]{2,1,0:T(8,128)(2,1)} %param.15), kind=kOutput, calls=%fused_computation.4 | convolution fusion | flops 6442450944 | bytes 23068672 | tf_op jit(solution)/shard_map/dot_general | solution.py:135
  128.4 25.1 %fusion.6 = bf16[384,4096]{1,0:T(8,128)(2,1)S(1)} fusion(bf16[1,2048,4096]{2,1,0:T(8,128)(2,1)} %param.17, f32[384,2048]{1,0:T(8,128)} %fusion.4, bf16[384,4096]{1,0:T(8,128)(2,1)} %copy-done.3, bf16[1,4096,2048]{2,1,0:T(8,128)(2,1)} %param.16), kind=kOutput, calls=%fused_computation.7 | convolution fusion | flops 12891193344 | bytes 42991616 | tf_op jit(solution)/shard_map/dot_general | solution.py:138
  153.5 4.5 %multiply_convert_fusion = bf16[512,4096]{1,0:T(8,128)(2,1)} fusion(bf16[384,4096]{1,0:T(8,128)(2,1)S(1)} %fusion.6, f32[512]{0:T(512)S(1)} %add.19, s32[512]{0:T(512)S(1)} %convert_select_fusion), kind=kOutput, calls=%fused_computation.6 | convolution fusion | flops 1615003648 | bytes 7344128 | tf_op jit(solution)/shard_map/dot_general | solution.py:139
  158.0 0.0 reduce-scatter.2.cloned.1.call-update
  158.0 37.1 %shard_map.105 = bf16[128,8192]{1,0:T(8,128)(2,1)} custom-call(s32[1]{0:T(128)} %bitcast.me_ref, bf16[64,128,576]{2,1,0:T(8,128)(2,1)} %bitcast.25, bf16[2048,576]{1,0:T(8,128)(2,1)} %all-gather.3.cloned.1.call-done.kv_ref, bf16[64,512,128]{2,1,0:T(8,128)(2,1)} %wv_ref.3, bf16[128,8192]{1,0:T(8,128)(2,1)} %shard_map.104.rest_0_), custom_call_target="tpu_custom_call", output_to_operand_aliasing={{}: (4, {})} | custom-call | flops 18253611008 | bytes 8912896 | tf_op jit(solution)/shard_map/pallas_call | solution.py:67
  195.1 34.4 %reduce-scatter.2.cloned.1.call-done = bf16[32,4096]{1,0:T(8,128)(2,1)} async-done(((bf16[512,4096]{1,0:T(8,128)(2,1)}), bf16[32,4096]{1,0:T(8,128)(2,1)}) %reduce-scatter.2.cloned.1.call-update) | async-done | bytes 262160 | tf_op jit(solution)/shard_map/reduce_scatter | solution.py:147
  (16 shorter events, 0.1 us)
Async XLA Ops:
  7.2 2.6 %copy-start = (bf16[4096,16]{0,1:T(8,128)(2,1)S(1)}, bf16[4096,16]{0,1:T(8,128)(2,1)}, u32[]{:S(2)}) copy-start(bf16[4096,16]{0,1:T(8,128)(2,1)} %param.14) | copy-start | bytes 393220
  7.2 49.5 %all-gather.3.cloned.1.call-start = ((), (), s32[]{:S(2)}) async-start(), calls=%async_computation.1 | async-start | bytes 2785280 | tf_op jit(solution)/shard_map/all_gather | solution.py:98
  9.0 100.1 %all-gather.5.cloned.1.call-start = ((), (), s32[]{:S(2)}) async-start(), calls=%async_computation.2 | async-start | bytes 4595712 | tf_op jit(solution)/shard_map/all_gather | solution.py:112
  11.1 14.1 %copy-start.2 = (bf16[32,4096]{1,0:T(8,128)(2,1)S(1)}, bf16[32,4096]{1,0:T(8,128)(2,1)}, u32[]{:S(2)}) copy-start(bf16[32,4096]{1,0:T(8,128)(2,1)} %param.12) | copy-start | bytes 786436
  56.7 172.8 %reduce-scatter.2.cloned.1.call-start = ((), (), s32[]{:S(2)}) async-start(), calls=%async_computation.3 | async-start | bytes 4456448 | tf_op jit(solution)/shard_map/reduce_scatter | solution.py:147
  114.7 1.6 copy-start.3
  158.0 71.5 %copy-start.1 = (bf16[4096,16]{0,1:T(8,128)(2,1)S(1)}, bf16[4096,16]{0,1:T(8,128)(2,1)}, u32[]{:S(2)}) copy-start(bf16[4096,16]{0,1:T(8,128)(2,1)} %param.14) | copy-start | bytes 393220
Sparse Core Ops, SparseCore 0:
  10.8 45.7 all-gather.2
  59.0 50.0 all-gather.4
  158.1 71.3 reduce-scatter.1
where the time goes:
time: 237 us; the launch traced here: 236 us
  waiting for transfers between devices  80.7 us (34%)
  Pallas kernels  73.9 us (31%)
  matrix products  47 us (20%)
  local copies, waits for them, and re-layouts  17.6 us (7%)
  between operations  13.9 us (6%)
  other arithmetic  2.85 us (1%)
    pallas_call x2, Pallas kernels, attend(): pl.pallas_call(functools.partial(attend_kernel, per_sub, scale), grid=(co...  73.9 us
    reduce_scatter x1, waiting for transfers between devices, per_device(): lax.psum_scatter(contributions, 'ep', scatter_dimension=0, tiled=True)  34.4 us
    all_gather x1, waiting for transfers between devices, per_device(): kv = lax.all_gather(latent_kv, 'ep', axis=0, tiled=True)  30.8 us
    dot_general x1, matrix products, per_device(): jnp.dot(hidden, w_down[j], preferred_element_type=jnp.float32)  25.1 us
    unnamed x11, local copies, waits for them, and re-layouts  17.6 us
    all_gather x1, waiting for transfers between devices, per_device(): packed = lax.all_gather(outgoing, 'ep', axis=0, tiled=True)  15.5 us
    dot_general x1, matrix products, per_device(): gate = jnp.dot(rows, w_gate[j], preferred_element_type=jnp.float32)  12 us
  transfers between devices with their start and end apart: 3, of which 3 were waited for; matrix products, arithmetic and copies ran while one was open for 7% of the time, Pallas kernels for 31%

commit v1 on v0

v1 whole, which is shorter than its diff:
```python
import functools

import jax
import jax.numpy as jnp
from jax import lax
from jax.experimental import pallas as pl
from jax.experimental.pallas import tpu as pltpu
from jax.sharding import PartitionSpec as P

ROUTED_SCALE = 2.5
NEGATIVE = -1e30
LOG2E = 1.4426950408889634
MESH = pl.DeviceIdType.MESH
F32 = jnp.float32
BF16 = jnp.bfloat16
LANES = 128
UP_SLOTS = 3
DOWN_SLOTS = 3
MOE_AT = 6


def layer_kernel(dims, q_ref, kv_ref, wv_ref, tok_ref, routes_ref, router_ref, wg_ref, wu_ref,
                 wd_ref, out_ref, moe_ref, *scratch):
    (zs, heads, width, latent, vdim, seq_dev, tb, model, ff, experts, cap, scale, ufc, fc) = dims
    (kvt_all, kv_all, q_a, q_b, s_a, s_b, m_a, m_b, l_a, l_b, acc_a, acc_b, wv_a, wv_b, tok_all,
     aux, rows, hidden, chosen_t, gate_col, contrib, recv1, part2, recv2, part3, recv3, wg_buf,
     wu_buf, wd_buf, q_sem, wv_sem, own_sem, kv_send, kv_recv, tok_send, tok_recv, wg_sem, wu_sem,
     wd_sem, s1_send, s1_recv, s2_send, s2_recv, s3_send, s3_recv) = scratch
    me = lax.axis_index("ep")
    z = me // 4
    x = lax.rem(me // 2, 2)
    c = lax.rem(me, 2)
    chunk = 4 * seq_dev
    pairs = heads // 2
    turns = pairs // 2
    moe_at = min(MOE_AT, turns - 1)
    group = 2 * zs * tb
    group_slots = 2 * zs * cap
    up_steps = ff // ufc
    down_steps = model // fc
    factor = scale * LOG2E

    def at(zz, xx, cc):
        return {"ep": zz * 4 + xx * 2 + cc}

    peers = [at(lax.rem(z + d, zs), x, c) for d in range(1, zs)]
    across = at(z, 1 - x, c)
    partner = at(z, x, 1 - c)

    own_kv = pltpu.make_async_copy(
        kv_ref,
        kvt_all.at[z, pl.ds(0, width), pl.ds(pl.multiple_of((x * 2 + c) * seq_dev, seq_dev), seq_dev)],
        own_sem.at[0],
    )
    own_kv.start()

    def block_row(zz, xx):
        return pl.multiple_of((xx * zs + zz) * tb, tb)

    own_tok = pltpu.make_async_copy(
        tok_ref, tok_all.at[c, pl.ds(block_row(z, x), tb), pl.ds(0, model)], own_sem.at[1]
    )
    own_tok.start()

    def q_copies(pair, buf, slot, base):
        return [
            pltpu.make_async_copy(
                q_ref.at[2 * pair + h],
                buf.at[slot, pl.ds(0, width), pl.ds(h * seq_dev, seq_dev)],
                q_sem.at[base, slot, h],
            )
            for h in range(2)
        ]

    def wv_copy(pair, buf, slot, base):
        return pltpu.make_async_copy(
            wv_ref.at[pl.ds(2 * pair, 2)], buf.at[slot], wv_sem.at[base, slot]
        )

    for copy in q_copies(0, q_a, 0, 0) + q_copies(1, q_b, 0, 1):
        copy.start()

    def up_copies(n):
        slot = lax.rem(n, UP_SLOTS)
        cols = pl.ds(pl.multiple_of(n * ufc, ufc), ufc)
        return (
            pltpu.make_async_copy(wg_ref.at[0, :, cols], wg_buf.at[slot], wg_sem.at[slot]),
            pltpu.make_async_copy(wu_ref.at[0, :, cols], wu_buf.at[slot], wu_sem.at[slot]),
        )

    def down_copy(n):
        slot = lax.rem(n, DOWN_SLOTS)
        cols = pl.ds(pl.multiple_of(n * fc, fc), fc)
        return pltpu.make_async_copy(wd_ref.at[0, :, cols], wd_buf.at[slot], wd_sem.at[slot])

    barrier = pltpu.get_barrier_semaphore()
    for peer in peers + [across, partner]:
        pl.semaphore_signal(barrier, inc=1, device_id=peer, device_id_type=MESH)
    pl.semaphore_wait(barrier, zs + 1)

    def kv_block(zz, xx, cc):
        return kvt_all.at[
            zz, pl.ds(0, width), pl.ds(pl.multiple_of((xx * 2 + cc) * seq_dev, seq_dev), seq_dev)
        ]

    def kv_send_to(zz, xx, cc, target, index):
        block = kv_block(zz, xx, cc)
        return pltpu.make_async_remote_copy(
            src_ref=block,
            dst_ref=block,
            send_sem=kv_send.at[index],
            recv_sem=kv_recv.at[zz * 4 + xx * 2 + cc],
            device_id=target,
            device_id_type=MESH,
        )

    def kv_wait(zz, xx, cc):
        kv_send_to(zz, xx, cc, partner, 0).wait_recv()

    def kv_turn(zz, xx, cc):
        cols = pl.ds(pl.multiple_of((xx * 2 + cc) * seq_dev, seq_dev), seq_dev)
        at_row = pl.ds(pl.multiple_of((zz * 4 + xx * 2 + cc) * seq_dev, seq_dev), seq_dev)
        kv_all[at_row, :] = jnp.transpose(kvt_all[zz, :, cols])

    kvt_all[:, width:, :] = jnp.zeros((zs, kvt_all.shape[1] - width, chunk), BF16)
    for buf in (q_a, q_b):
        buf[:, width:, :] = jnp.zeros((2, buf.shape[1] - width, 2 * seq_dev), BF16)
    own_kv.wait()
    kv_send_to(z, x, c, across, zs - 1).start()
    kv_send_to(z, x, c, partner, 2 * zs - 1).start()
    for d in range(1, zs):

        @pl.when(z + d < zs)
        def _():
            kv_send_to(z, x, c, at(z + d, x, c), d - 1).start()

    own_tok.wait()

    own_rows = pl.ds(block_row(z, x), tb)
    logits = lax.dot_general(
        router_ref[...],
        tok_all[c, own_rows, :model],
        (((1,), (1,)), ((), ())),
        preferred_element_type=F32,
    )
    affinity = jax.nn.sigmoid(logits)
    expert_id = lax.broadcasted_iota(jnp.int32, (experts, tb), 0)
    named = jnp.zeros((experts, tb), F32)
    for k in range(routes_ref.shape[0]):
        named = jnp.where(routes_ref[k : k + 1, :] == expert_id, 1.0, named)
    kept = affinity * named
    gates = ROUTED_SCALE * kept / jnp.sum(kept, axis=0, keepdims=True)
    high = gates.astype(BF16).astype(F32)
    aux[...] = jnp.zeros(aux.shape, F32)
    aux[0:experts, 0:tb] = high
    aux[experts : 2 * experts, 0:tb] = gates - high
    aux[2 * experts : 3 * experts, 0:tb] = named
    tok_all[c, own_rows, model:] = jnp.transpose(aux[...])[:tb].astype(BF16)

    def tok_send_to(zz, xx, cc, target, index):
        block = tok_all.at[cc, pl.ds(block_row(zz, xx), tb)]
        return pltpu.make_async_remote_copy(
            src_ref=block,
            dst_ref=block,
            send_sem=tok_send.at[index],
            recv_sem=tok_recv.at[zz * 4 + xx * 2 + cc],
            device_id=target,
            device_id_type=MESH,
        )

    def tok_wait(zz, xx, cc):
        tok_send_to(zz, xx, cc, partner, 0).wait_recv()

    kv_turn(z, x, c)

    for d in range(1, zs):

        @pl.when(z - d >= 0)
        def _():
            kv_wait(z - d, x, c)
            kv_send_to(z - d, x, c, across, zs - 1 + d).start()
            kv_send_to(z - d, x, c, partner, 2 * zs - 1 + d).start()
            kv_turn(z - d, x, c)

    tok_send_to(z, x, c, across, zs - 1).start()
    for d in range(1, zs):
        tok_send_to(z, x, c, peers[d - 1], d - 1).start()
    tok_send_to(z, x, c, partner, 2 * zs - 1).start()

    for n in range(min(UP_SLOTS, up_steps)):
        for copy in up_copies(n):
            copy.start()
    for n in range(min(DOWN_SLOTS, down_steps)):
        down_copy(n).start()

    for d in range(zs):

        @pl.when(z - d >= 0)
        def _():
            kv_wait(z - d, 1 - x, c)
            kv_send_to(z - d, 1 - x, c, partner, 3 * zs - 1 + d).start()
            kv_turn(z - d, 1 - x, c)

    for d in range(zs):
        for xx in (x, 1 - x):

            @pl.when(z - d >= 0)
            def _():
                kv_wait(z - d, xx, 1 - c)
                kv_turn(z - d, xx, 1 - c)

    def scores_of(n, q, s, m, first):
        base = pl.multiple_of(n * chunk, chunk)
        score = jnp.dot(kv_all[pl.ds(base, chunk), :], q, preferred_element_type=F32)
        row = lax.broadcasted_iota(jnp.int32, score.shape, 0)
        col = lax.rem(lax.broadcasted_iota(jnp.int32, score.shape, 1), seq_dev)
        score = jnp.where(row - col <= me * seq_dev - base, score, NEGATIVE)
        s[pl.ds(base, chunk), :] = score
        high8 = jnp.max(score.reshape(chunk // 8, 8, score.shape[1]), axis=0)
        m[...] = high8 if first else jnp.maximum(m[...], high8)

    def values_of(n, s, m, l, acc, first):
        base = pl.multiple_of(n * chunk, chunk)
        top = jnp.max(m[...], axis=0, keepdims=True) * factor
        raised = jnp.exp2(s[pl.ds(base, chunk), :] * factor - top)
        sums = jnp.sum(raised.reshape(chunk // 8, 8, raised.shape[1]), axis=0)
        value = jnp.dot(kvt_all[n, :latent, :], raised.astype(BF16), preferred_element_type=F32)
        if first:
            l[...] = sums
            acc[...] = value
        else:
            l[...] += sums
            acc[...] += value

    def finish(pair, l, acc, wv, slot):
        totals = jnp.sum(l[...], axis=0, keepdims=True)
        context = (acc[...] * (1.0 / totals)).astype(BF16)
        for h in range(2):
            value = lax.dot_general(
                context[:, h * seq_dev : (h + 1) * seq_dev],
                wv[slot, h],
                (((0,), (0,)), ((), ())),
                preferred_element_type=F32,
            )
            cols = pl.ds(pl.multiple_of((2 * pair + h) * vdim, vdim), vdim)
            out_ref[:, cols] = value.astype(BF16)

    set_a = (q_a, s_a, m_a, l_a, acc_a, wv_a, 0)
    set_b = (q_b, s_b, m_b, l_b, acc_b, wv_b, 1)

    def half(i, cur, prev):
        q, s, m, l, acc, wv, parity = cur
        _, s_p, m_p, l_p, acc_p, _, _ = prev
        pair = 2 * i + parity
        slot = lax.rem(i, 2)
        other = 1 - slot
        for copy in q_copies(pair, q, slot, parity):
            copy.wait()

        @pl.when(i + 1 < turns)
        def _():
            for copy in q_copies(pair + 2, q, other, parity):
                copy.start()

        @pl.when(i >= 1)
        def _():
            wv_copy(pair - 2, wv, other, parity).wait()

        wv_copy(pair, wv, slot, parity).start()
        scores_of(0, q[slot], s, m, True)
        values_of(0, s_p, m_p, l_p, acc_p, True)
        finish(jnp.maximum(pair - 2, 0), l, acc, wv, other)

        def more(n, carry):
            scores_of(n, q[slot], s, m, False)
            values_of(n, s_p, m_p, l_p, acc_p, False)
            return carry

        lax.fori_loop(1, z + 1, more, 0)

    def from_peer(d):
        zz = lax.rem(z + d, zs)
        tok_wait(zz, x, c)
        tok_send_to(zz, x, c, across, zs - 1 + d).start()
        tok_send_to(zz, x, c, partner, 2 * zs - 1 + d).start()

    def from_across(d):
        zz = lax.rem(z + d, zs)
        tok_wait(zz, 1 - x, c)
        tok_send_to(zz, 1 - x, c, partner, 3 * zs - 1 + d).start()

    def from_partner():
        for d in range(zs):
            for xx in (x, 1 - x):
                tok_wait(lax.rem(z + d, zs), xx, 1 - c)

    gather_steps = [functools.partial(from_across, 0)]
    gather_steps += [functools.partial(from_peer, d) for d in range(1, zs)]
    gather_steps += [functools.partial(from_across, d) for d in range(1, zs)]
    gather_steps += [from_partner]
    spots = [
        (2 * moe_at * (a + 1)) // len(gather_steps) for a in range(len(gather_steps))
    ]

    def features(k):
        return pl.ds(pl.multiple_of(k * fc, fc), fc)

    half_rows = group // 2

    def first_copy(k):
        return pltpu.make_async_remote_copy(
            src_ref=contrib.at[1 - c, :, features(k)],
            dst_ref=recv1.at[:, features(k)],
            send_sem=s1_send.at[k],
            recv_sem=s1_recv.at[k],
            device_id=partner,
            device_id_type=MESH,
        )

    def second_copy(k):
        away = pl.ds(pl.multiple_of((1 - x) * half_rows, half_rows), half_rows)
        return pltpu.make_async_remote_copy(
            src_ref=part2.at[away, features(k)],
            dst_ref=recv2.at[:, features(k)],
            send_sem=s2_send.at[k],
            recv_sem=s2_recv.at[k],
            device_id=across,
            device_id_type=MESH,
        )

    def third_copy(k, d):
        to = lax.rem(z + d, zs)
        return pltpu.make_async_remote_copy(
            src_ref=part3.at[pl.ds(pl.multiple_of(to * tb, tb), tb), features(k)],
            dst_ref=recv3.at[d - 1, :, features(k)],
            send_sem=s3_send.at[k, d - 1],
            recv_sem=s3_recv.at[k, d - 1],
            device_id=peers[d - 1],
            device_id_type=MESH,
        )

    def second_step(k):
        first_copy(k).wait_recv()
        total = contrib[c, :, features(k)].astype(F32) + recv1[:, features(k)].astype(F32)
        part2[:, features(k)] = total.astype(BF16)
        second_copy(k).start()

    def third_step(k):
        second_copy(k).wait_recv()
        mine = pl.ds(pl.multiple_of(x * half_rows, half_rows), half_rows)
        total = part2[mine, features(k)].astype(F32) + recv2[:, features(k)].astype(F32)
        part3[:, features(k)] = total.astype(BF16)
        for d in range(1, zs):
            third_copy(k, d).start()

    def last_step(k):
        mine = pl.ds(pl.multiple_of(z * tb, tb), tb)
        total = part3[mine, features(k)].astype(F32)
        for d in range(1, zs):
            third_copy(k, d).wait_recv()
            total = total + recv3[d - 1, :, features(k)].astype(F32)
        moe_ref[:, features(k)] = total.astype(BF16)

    def expert():
        lane = lax.broadcasted_iota(jnp.int32, (group, LANES), 1)
        row = lax.broadcasted_iota(jnp.int32, (group, group), 0)
        col = lax.broadcasted_iota(jnp.int32, (group, group), 1)
        before = jnp.where((col < row) & (col // tb == row // tb), 1.0, 0.0).astype(BF16)
        slot_of = lax.broadcasted_iota(jnp.int32, (group, group_slots), 1)
        block = lax.broadcasted_iota(jnp.int32, (group, group_slots), 0) // tb
        wide = min(1024, model)
        for g in range(2):
            extra = tok_all[g, :, model:]
            value = extra.astype(F32)
            gate = (lane == me) | (lane == experts + me)
            gate_col[g] = jnp.sum(jnp.where(gate, value, 0.0), axis=1, keepdims=True)
            pick = lane == 2 * experts + me
            member = jnp.sum(jnp.where(pick, value, 0.0), axis=1, keepdims=True)
            ranks = jnp.dot(before, extra, preferred_element_type=F32)
            rank = jnp.sum(jnp.where(pick, ranks, 0.0), axis=1, keepdims=True)
            target = block.astype(F32) * cap + rank
            chosen = jnp.where((member > 0.5) & (target == slot_of.astype(F32)), 1.0, 0.0)
            chosen_t[g] = chosen.astype(BF16)
            picked = jnp.transpose(chosen).astype(BF16)

            def take(n, carry):
                cols = pl.ds(pl.multiple_of(n * wide, wide), wide)
                rows[g * group_slots : (g + 1) * group_slots, cols] = jnp.dot(
                    picked, tok_all[g, :, cols], preferred_element_type=F32
                ).astype(BF16)
                return carry

            lax.fori_loop(0, model // wide, take, 0)

        def up_step(n, carry):
            slot = lax.rem(n, UP_SLOTS)
            for copy in up_copies(n):
                copy.wait()
            gate = jnp.dot(rows[...], wg_buf[slot], preferred_element_type=F32)
            upward = jnp.dot(rows[...], wu_buf[slot], preferred_element_type=F32)
            value = (gate / (1.0 + jnp.exp(-gate)) * upward).astype(BF16)
            hidden[:, pl.ds(pl.multiple_of(n * ufc, ufc), ufc)] = value

            @pl.when(n + UP_SLOTS < up_steps)
            def _():
                for copy in up_copies(n + UP_SLOTS):
                    copy.start()

            return carry

        lax.fori_loop(0, up_steps, up_step, 0)

        def down_step(n, carry):
            down_copy(n).wait()
            slot = lax.rem(n, DOWN_SLOTS)
            value = jnp.dot(hidden[...], wd_buf[slot], preferred_element_type=F32).astype(BF16)
            for g in range(2):
                spread = jnp.dot(
                    chosen_t[g],
                    value[g * group_slots : (g + 1) * group_slots],
                    preferred_element_type=F32,
                )
                contrib[g, :, features(n)] = (spread * gate_col[g]).astype(BF16)

            @pl.when(n + DOWN_SLOTS < down_steps)
            def _():
                down_copy(n + DOWN_SLOTS).start()

            first_copy(n).start()

            @pl.when(n >= 1)
            def _():
                second_step(n - 1)

            return carry

        lax.fori_loop(0, down_steps, down_step, 0)
        second_step(down_steps - 1)

    def gather_at(i, parity):
        for step, spot in zip(gather_steps, spots):
            if spot % 2 == parity:
                pl.when(i == spot // 2)(step)

    def turn(i, carry):
        gather_at(i, 0)
        pl.when(i == moe_at)(expert)

        @pl.when((i >= moe_at + 3) & (i < moe_at + 3 + down_steps))
        def _():
            last_step(i - moe_at - 3)

        half(i, set_a, set_b)
        gather_at(i, 1)

        @pl.when((i >= moe_at) & (i < moe_at + down_steps))
        def _():
            third_step(i - moe_at)

        half(i, set_b, set_a)
        return carry

    lax.fori_loop(0, turns, turn, 0)

    slot = (turns - 1) % 2
    wv_copy(pairs - 2, wv_a, slot, 0).wait()
    values_of(0, s_b, m_b, l_b, acc_b, True)
    finish(pairs - 2, l_a, acc_a, wv_a, slot)

    def rest(n, carry):
        values_of(n, s_b, m_b, l_b, acc_b, False)
        return carry

    lax.fori_loop(1, z + 1, rest, 0)
    wv_copy(pairs - 1, wv_b, slot, 1).wait()
    finish(pairs - 1, l_b, acc_b, wv_b, slot)

    third_done = min(max(turns - moe_at, 0), down_steps)
    last_done = min(max(turns - moe_at - 3, 0), down_steps)

    def third_rest(k, carry):
        third_step(k)
        return carry

    def last_rest(k, carry):
        last_step(k)
        return carry

    lax.fori_loop(third_done, down_steps, third_rest, 0)
    lax.fori_loop(last_done, down_steps, last_rest, 0)

    for d in range(1, zs):

        @pl.when(z + d < zs)
        def _():
            kv_send_to(z, x, c, partner, d - 1).wait_send()

    for d in range(zs):

        @pl.when(z - d >= 0)
        def _():
            for base in (zs - 1, 2 * zs - 1, 3 * zs - 1):
                kv_send_to(z, x, c, partner, base + d).wait_send()

    for index in range(4 * zs - 1):
        tok_send_to(z, x, c, partner, index).wait_send()

    def drain(k, carry):
        first_copy(k).wait_send()
        second_copy(k).wait_send()
        for d in range(1, zs):
            third_copy(k, d).wait_send()
        return carry

    lax.fori_loop(0, down_steps, drain, 0)


def per_device(queries, latent_kv, w_value, moe_tokens, routes, router, w_gate, w_up, w_down):
    seq_dev, heads, width = queries.shape
    latent, vdim = w_value.shape[1], w_value.shape[2]
    scale = (vdim + width - latent) ** (-0.5)
    tb, top = routes.shape
    ep_size = lax.axis_size("ep")
    experts = router.shape[1]
    assert experts == ep_size and w_gate.shape[0] == 1 and ep_size % 4 == 0
    model, ff = moe_tokens.shape[1], w_gate.shape[2]
    cap = min(tb, 3 * tb * top // (2 * experts))
    zs = ep_size // 4
    wide = -(-width // LANES) * LANES
    keys = ep_size * seq_dev
    group, group_slots = ep_size * tb // 2, ep_size * cap // 2
    ufc = min(256, ff)
    fc = min(512, model)
    down_steps = model // fc
    dims = (zs, heads, width, latent, vdim, seq_dev, tb, model, ff, experts, cap, scale, ufc, fc)
    cols = 2 * seq_dev
    vmem, dma = pltpu.VMEM, pltpu.SemaphoreType.DMA
    scratch = [
        vmem((zs, wide, 4 * seq_dev), BF16),
        vmem((keys, wide), BF16),
        vmem((2, wide, cols), BF16),
        vmem((2, wide, cols), BF16),
        vmem((keys, cols), F32),
        vmem((keys, cols), F32),
        vmem((8, cols), F32),
        vmem((8, cols), F32),
        vmem((8, cols), F32),
        vmem((8, cols), F32),
        vmem((latent, cols), F32),
        vmem((latent, cols), F32),
        vmem((2, 2, latent, vdim), BF16),
        vmem((2, 2, latent, vdim), BF16),
        vmem((2, group, model + LANES), BF16),
        vmem((LANES, LANES), F32),
        vmem((2 * group_slots, model), BF16),
        vmem((2 * group_slots, ff), BF16),
        vmem((2, group, group_slots), BF16),
        vmem((2, group, 1), F32),
        vmem((2, group, model), BF16),
        vmem((group, model), BF16),
        vmem((group, model), BF16),
        vmem((group // 2, model), BF16),
        vmem((group // 2, model), BF16),
        vmem((zs - 1, tb, model), BF16),
        vmem((UP_SLOTS, model, ufc), BF16),
        vmem((UP_SLOTS, model, ufc), BF16),
        vmem((DOWN_SLOTS, ff, fc), BF16),
        dma((2, 2, 2)),
        dma((2, 2)),
        dma((2,)),
        dma((4 * zs - 1,)),
        dma((4 * zs,)),
        dma((4 * zs - 1,)),
        dma((4 * zs,)),
        dma((UP_SLOTS,)),
        dma((UP_SLOTS,)),
        dma((DOWN_SLOTS,)),
        dma((down_steps,)),
        dma((down_steps,)),
        dma((down_steps,)),
        dma((down_steps,)),
        dma((down_steps, zs - 1)),
        dma((down_steps, zs - 1)),
    ]
    hbm = pl.BlockSpec(memory_space=pl.ANY)
    local = pl.BlockSpec(memory_space=pltpu.VMEM)
    attention_out, moe_out = pl.pallas_call(
        functools.partial(layer_kernel, dims),
        in_specs=[hbm, hbm, hbm, hbm, local, local, hbm, hbm, hbm],
        out_specs=[local, local],
        out_shape=[
            jax.ShapeDtypeStruct((seq_dev, heads * vdim), BF16),
            jax.ShapeDtypeStruct((tb, model), BF16),
        ],
        scratch_shapes=scratch,
        compiler_params=pltpu.CompilerParams(
            vmem_limit_bytes=67043328, collective_id=0, has_side_effects=True
        ),
        cost_estimate=pl.CostEstimate(
            flops=heads * seq_dev * keys * (width + latent) * 2,
            bytes_accessed=6 * model * ff,
            transcendentals=heads * seq_dev * keys,
        ),
    )(
        jnp.transpose(queries, (1, 2, 0)),
        jnp.transpose(latent_kv),
        w_value,
        moe_tokens,
        jnp.transpose(routes),
        jnp.transpose(router),
        w_gate,
        w_up,
        w_down,
    )
    if lax.axis_size("node") > 1:
        moe_out = lax.psum_scatter(moe_out, "node", scatter_dimension=1, tiled=True)
    return (attention_out, moe_out)


def solution(mesh):
    placed = (
        P(("groups", "ep"), "node", None),
        P(("groups", "ep"), None),
        P("node", None, None),
        P(("groups", "ep"), None),
        P(("groups", "ep"), None),
        P(),
        P("ep", None, "node"),
        P("ep", None, "node"),
        P("ep", "node", None),
    )
    return jax.shard_map(
        per_device,
        mesh=mesh,
        in_specs=placed,
        out_specs=(P(("groups", "ep"), "node"), P(("groups", "ep"), "node")),
        check_vma=False,
    )
```

time: 237 us -> 142 us (0.60)
  the two profiles are of different devices: /device:TPU:0 before, /device:TPU:29 now
where the time goes in v1:
time: 142 us
  Pallas kernels  136 us (96%)
  local copies, waits for them, and re-layouts  4.76 us (3%)
    pallas_call x1, Pallas kernels, per_device(): pl.pallas_call(functools.partial(layer_kernel, dims), in_specs=[hbm, hbm,...  136 us
    unnamed x2, local copies, waits for them, and re-layouts  4.76 us

profile of v1, /device:TPU:29, one launch (start us, length us, event | category | flops | bytes accessed | tf_op | source)
XLA Modules:
  0.0 141.8 jit_solution(9696326693788160078)
XLA Ops:
  0.6 136.4 %shard_map.104 = (bf16[128,8192]{1,0:T(8,128)(2,1)}, bf16[32,4096]{1,0:T(8,128)(2,1)}) custom-call(bf16[64,576,128]{2,1,0:T(8,128)(2,1)} %bitcast.4, bf16[576,128]{1,0:T(8,128)(2,1)} %bitcast.5, bf16[64,512,128]{2,1,0:T(8,128)(2,1)} %wv_ref.1, bf16[32,4096]{1,0:T(8,128)(2,1)} %tok_ref.1, s32[8,32]{1,0:T(8,128)} %bitcast.7, bf16[16,4096]{1,0:T(8,128)(2,1)} %bitcast.6, ...), custom_call_target="tpu_custom_call" | custom-call | flops 36507222016 | bytes 50331648 | tf_op jit(solution)/shard_map/pallas_call | solution.py:587
  137.1 3.1 %copy.13 = bf16[128,8192]{1,0:T(8,128)(2,1)} copy(bf16[128,8192]{1,0:T(8,128)(2,1)} %get-tuple-element.4) | data formatting | bytes 4194304
  140.2 1.7 %copy.14 = bf16[32,4096]{1,0:T(8,128)(2,1)} copy(bf16[32,4096]{1,0:T(8,128)(2,1)} %get-tuple-element.5) | data formatting | bytes 524288

commit v2 on v1

--- a/solution.py
+++ b/solution.py
@@ -14,14 +14,15 @@
 F32 = jnp.float32
 BF16 = jnp.bfloat16
 LANES = 128
-UP_SLOTS = 3
-DOWN_SLOTS = 3
-MOE_AT = 6
+UP_SLOTS = 2
+DOWN_SLOTS = 2
+MOE_AT = 7
 
 
 def layer_kernel(dims, q_ref, kv_ref, wv_ref, tok_ref, routes_ref, router_ref, wg_ref, wu_ref,
                  wd_ref, out_ref, moe_ref, *scratch):
-    (zs, heads, width, latent, vdim, seq_dev, tb, model, ff, experts, cap, scale, ufc, fc) = dims
+    (zs, heads, width, latent, vdim, seq_dev, tb, model, ff, experts, cap, scale, ufc, dfc,
+     fc) = dims
     (kvt_all, kv_all, q_a, q_b, s_a, s_b, m_a, m_b, l_a, l_b, acc_a, acc_b, wv_a, wv_b, tok_all,
      aux, rows, hidden, chosen_t, gate_col, contrib, recv1, part2, recv2, part3, recv3, wg_buf,
      wu_buf, wd_buf, q_sem, wv_sem, own_sem, kv_send, kv_recv, tok_send, tok_recv, wg_sem, wu_sem,
@@ -37,7 +38,9 @@
     group = 2 * zs * tb
     group_slots = 2 * zs * cap
     up_steps = ff // ufc
-    down_steps = model // fc
+    down_steps = model // dfc
+    send_steps = model // fc
+    per_down = dfc // fc
     factor = scale * LOG2E
 
     def at(zz, xx, cc):
@@ -90,7 +93,7 @@
 
     def down_copy(n):
         slot = lax.rem(n, DOWN_SLOTS)
-        cols = pl.ds(pl.multiple_of(n * fc, fc), fc)
+        cols = pl.ds(pl.multiple_of(n * dfc, dfc), dfc)
         return pltpu.make_async_copy(wd_ref.at[0, :, cols], wd_buf.at[slot], wd_sem.at[slot])
 
     barrier = pltpu.get_barrier_semaphore()
@@ -126,13 +129,14 @@
     for buf in (q_a, q_b):
         buf[:, width:, :] = jnp.zeros((2, buf.shape[1] - width, 2 * seq_dev), BF16)
     own_kv.wait()
+    def kv_up(d):
+        @pl.when(z + 1 < zs)
+        def _():
+            kv_send_to(z - d, x, c, at(z + 1, x, c), d).start()
+
+    kv_up(0)
     kv_send_to(z, x, c, across, zs - 1).start()
     kv_send_to(z, x, c, partner, 2 * zs - 1).start()
-    for d in range(1, zs):
-
-        @pl.when(z + d < zs)
-        def _():
-            kv_send_to(z, x, c, at(z + d, x, c), d - 1).start()
 
     own_tok.wait()
 
@@ -178,14 +182,29 @@
         @pl.when(z - d >= 0)
         def _():
             kv_wait(z - d, x, c)
+            if d < zs - 1:
+                kv_up(d)
             kv_send_to(z - d, x, c, across, zs - 1 + d).start()
             kv_send_to(z - d, x, c, partner, 2 * zs - 1 + d).start()
             kv_turn(z - d, x, c)
 
-    tok_send_to(z, x, c, across, zs - 1).start()
-    for d in range(1, zs):
-        tok_send_to(z, x, c, peers[d - 1], d - 1).start()
-    tok_send_to(z, x, c, partner, 2 * zs - 1).start()
+    def tok_up(d):
+        @pl.when(z + 1 < zs)
+        def _():
+            tok_send_to(z - d, x, c, at(z + 1, x, c), 3 * zs + d).start()
+
+    def tok_down(d):
+        @pl.when(z > 0)
+        def _():
+            tok_send_to(z + d, x, c, at(z - 1, x, c), 4 * zs - 1 + d).start()
+
+    def tok_aside(zz):
+        tok_send_to(zz, x, c, across, zz).start()
+        tok_send_to(zz, x, c, partner, zs + zz).start()
+
+    tok_up(0)
+    tok_down(0)
+    tok_aside(z)
 
     for n in range(min(UP_SLOTS, up_steps)):
         for copy in up_copies(n):
@@ -209,28 +228,40 @@
                 kv_wait(z - d, xx, 1 - c)
                 kv_turn(z - d, xx, 1 - c)
 
-    def scores_of(n, q, s, m, first):
-        base = pl.multiple_of(n * chunk, chunk)
-        score = jnp.dot(kv_all[pl.ds(base, chunk), :], q, preferred_element_type=F32)
-        row = lax.broadcasted_iota(jnp.int32, score.shape, 0)
-        col = lax.rem(lax.broadcasted_iota(jnp.int32, score.shape, 1), seq_dev)
-        score = jnp.where(row - col <= me * seq_dev - base, score, NEGATIVE)
-        s[pl.ds(base, chunk), :] = score
-        high8 = jnp.max(score.reshape(chunk // 8, 8, score.shape[1]), axis=0)
-        m[...] = high8 if first else jnp.maximum(m[...], high8)
-
-    def values_of(n, s, m, l, acc, first):
-        base = pl.multiple_of(n * chunk, chunk)
-        top = jnp.max(m[...], axis=0, keepdims=True) * factor
-        raised = jnp.exp2(s[pl.ds(base, chunk), :] * factor - top)
+    def scores_of(n, q, s, diagonal):
+        base = n * chunk
+        score = jnp.dot(kv_all[base : base + chunk, :], q, preferred_element_type=F32)
+        if diagonal:
+            row = lax.broadcasted_iota(jnp.int32, score.shape, 0)
+            col = lax.rem(lax.broadcasted_iota(jnp.int32, score.shape, 1), seq_dev)
+            score = jnp.where(row - col <= (x * 2 + c) * seq_dev, score, NEGATIVE)
+        s[base : base + chunk, :] = score
+        return jnp.max(score.reshape(chunk // 8, 8, score.shape[1]), axis=0)
+
+    def values_of(n, s, high):
+        base = n * chunk
+        raised = jnp.exp2(s[base : base + chunk, :] * factor - high)
         sums = jnp.sum(raised.reshape(chunk // 8, 8, raised.shape[1]), axis=0)
         value = jnp.dot(kvt_all[n, :latent, :], raised.astype(BF16), preferred_element_type=F32)
-        if first:
-            l[...] = sums
-            acc[...] = value
-        else:
-            l[...] += sums
-            acc[...] += value
+        return sums, value
+
+    def sweep(top, q, s, m, s_p, m_p, l_p, acc_p):
+        if s_p is not None:
+            high = jnp.max(m_p[...], axis=0, keepdims=True) * factor
+        tops = sums = value = None
+        for n in [top] + list(range(top)):
+            if s is not None:
+                high8 = scores_of(n, q, s, n == top)
+                tops = high8 if tops is None else jnp.maximum(tops, high8)
+            if s_p is not None:
+                sums_n, value_n = values_of(n, s_p, high)
+                sums = sums_n if sums is None else sums + sums_n
+                value = value_n if value is None else value + value_n
+        if s is not None:
+            m[...] = tops
+        if s_p is not None:
+            l_p[...] = sums
+            acc_p[...] = value
 
     def finish(pair, l, acc, wv, slot):
         totals = jnp.sum(l[...], axis=0, keepdims=True)
@@ -267,39 +298,50 @@
             wv_copy(pair - 2, wv, other, parity).wait()
 
         wv_copy(pair, wv, slot, parity).start()
-        scores_of(0, q[slot], s, m, True)
-        values_of(0, s_p, m_p, l_p, acc_p, True)
-        finish(jnp.maximum(pair - 2, 0), l, acc, wv, other)
-
-        def more(n, carry):
-            scores_of(n, q[slot], s, m, False)
-            values_of(n, s_p, m_p, l_p, acc_p, False)
-            return carry
-
-        lax.fori_loop(1, z + 1, more, 0)
-
-    def from_peer(d):
-        zz = lax.rem(z + d, zs)
-        tok_wait(zz, x, c)
-        tok_send_to(zz, x, c, across, zs - 1 + d).start()
-        tok_send_to(zz, x, c, partner, 2 * zs - 1 + d).start()
+        for top in range(zs):
+
+            @pl.when(z == top)
+            def _():
+                sweep(top, q[slot], s, m, s_p, m_p, l_p, acc_p)
+                finish(jnp.maximum(pair - 2, 0), l, acc, wv, other)
+
+    def from_levels(d):
+        @pl.when(z - d >= 0)
+        def _():
+            tok_wait(z - d, x, c)
+            if d < zs - 1:
+                tok_up(d)
+            tok_aside(z - d)
+
+        @pl.when(z + d < zs)
+        def _():
+            tok_wait(z + d, x, c)
+            if d < zs - 1:
+                tok_down(d)
+            tok_aside(z + d)
+
+    def pass_on(zz):
+        tok_wait(zz, 1 - x, c)
+        tok_send_to(zz, 1 - x, c, partner, 2 * zs + zz).start()
 
     def from_across(d):
-        zz = lax.rem(z + d, zs)
-        tok_wait(zz, 1 - x, c)
-        tok_send_to(zz, 1 - x, c, partner, 3 * zs - 1 + d).start()
+        if d == 0:
+            pass_on(z)
+        else:
+            pl.when(z - d >= 0)(lambda: pass_on(z - d))
+            pl.when(z + d < zs)(lambda: pass_on(z + d))
 
     def from_partner():
         for d in range(zs):
             for xx in (x, 1 - x):
                 tok_wait(lax.rem(z + d, zs), xx, 1 - c)
 
-    gather_steps = [functools.partial(from_across, 0)]
-    gather_steps += [functools.partial(from_peer, d) for d in range(1, zs)]
-    gather_steps += [functools.partial(from_across, d) for d in range(1, zs)]
-    gather_steps += [from_partner]
+    gather_steps = []
+    for d in range(1, zs):
+        gather_steps += [functools.partial(from_levels, d), functools.partial(from_across, d - 1)]
+    gather_steps += [functools.partial(from_across, zs - 1), from_partner]
     spots = [
-        (2 * moe_at * (a + 1)) // len(gather_steps) for a in range(len(gather_steps))
+        (2 * moe_at * a) // (len(gather_steps) - 1) for a in range(len(gather_steps))
     ]
 
     def features(k):
@@ -420,22 +462,26 @@
                     value[g * group_slots : (g + 1) * group_slots],
                     preferred_element_type=F32,
                 )
-                contrib[g, :, features(n)] = (spread * gate_col[g]).astype(BF16)
+                whole = pl.ds(pl.multiple_of(n * dfc, dfc), dfc)
+                contrib[g, :, whole] = (spread * gate_col[g]).astype(BF16)
 
             @pl.when(n + DOWN_SLOTS < down_steps)
             def _():
                 down_copy(n + DOWN_SLOTS).start()
 
-            first_copy(n).start()
+            for k in range(per_down):
+                first_copy(n * per_down + k).start()
 
             @pl.when(n >= 1)
             def _():
-                second_step(n - 1)
+                for k in range(per_down):
+                    second_step((n - 1) * per_down + k)
 
             return carry
 
         lax.fori_loop(0, down_steps, down_step, 0)
-        second_step(down_steps - 1)
+        for k in range(send_steps - per_down, send_steps):
+            second_step(k)
 
     def gather_at(i, parity):
         for step, spot in zip(gather_steps, spots):
@@ -446,14 +492,14 @@
         gather_at(i, 0)
         pl.when(i == moe_at)(expert)
 
-        @pl.when((i >= moe_at + 3) & (i < moe_at + 3 + down_steps))
+        @pl.when((i >= moe_at + 3) & (i < moe_at + 3 + send_steps))
         def _():
             last_step(i - moe_at - 3)
 
         half(i, set_a, set_b)
         gather_at(i, 1)
 
-        @pl.when((i >= moe_at) & (i < moe_at + down_steps))
+        @pl.when((i >= moe_at) & (i < moe_at + send_steps))
         def _():
             third_step(i - moe_at)
 
@@ -464,19 +510,17 @@
 
     slot = (turns - 1) % 2
     wv_copy(pairs - 2, wv_a, slot, 0).wait()
-    values_of(0, s_b, m_b, l_b, acc_b, True)
     finish(pairs - 2, l_a, acc_a, wv_a, slot)
-
-    def rest(n, carry):
-        values_of(n, s_b, m_b, l_b, acc_b, False)
-        return carry
-
-    lax.fori_loop(1, z + 1, rest, 0)
+    for top in range(zs):
+        pl.when(z == top)(
+            functools.partial(sweep, top, None, None, None, s_b, m_b, l_b, acc_b)
+        )
+
     wv_copy(pairs - 1, wv_b, slot, 1).wait()
     finish(pairs - 1, l_b, acc_b, wv_b, slot)
 
-    third_done = min(max(turns - moe_at, 0), down_steps)
-    last_done = min(max(turns - moe_at - 3, 0), down_steps)
+    third_done = min(max(turns - moe_at, 0), send_steps)
+    last_done = min(max(turns - moe_at - 3, 0), send_steps)
 
     def third_rest(k, carry):
         third_step(k)
@@ -486,14 +530,22 @@
         last_step(k)
         return carry
 
-    lax.fori_loop(third_done, down_steps, third_rest, 0)
-    lax.fori_loop(last_done, down_steps, last_rest, 0)
-
-    for d in range(1, zs):
-
-        @pl.when(z + d < zs)
-        def _():
-            kv_send_to(z, x, c, partner, d - 1).wait_send()
+    lax.fori_loop(third_done, send_steps, third_rest, 0)
+    lax.fori_loop(last_done, send_steps, last_rest, 0)
+
+    for d in range(zs - 1):
+
+        @pl.when((z + 1 < zs) & (z - d >= 0))
+        def _():
+            kv_send_to(z, x, c, partner, d).wait_send()
+
+        @pl.when((z + 1 < zs) & (z - d >= 0))
+        def _():
+            tok_send_to(z, x, c, partner, 3 * zs + d).wait_send()
+
+        @pl.when((z > 0) & (z + d < zs))
+        def _():
+            tok_send_to(z, x, c, partner, 4 * zs - 1 + d).wait_send()
 
     for d in range(zs):
 
@@ -502,7 +554,7 @@
             for base in (zs - 1, 2 * zs - 1, 3 * zs - 1):
                 kv_send_to(z, x, c, partner, base + d).wait_send()
 
-    for index in range(4 * zs - 1):
+    for index in range(3 * zs):
         tok_send_to(z, x, c, partner, index).wait_send()
 
     def drain(k, carry):
@@ -512,7 +564,7 @@
             third_copy(k, d).wait_send()
         return carry
 
-    lax.fori_loop(0, down_steps, drain, 0)
+    lax.fori_loop(0, send_steps, drain, 0)
 
 
 def per_device(queries, latent_kv, w_value, moe_tokens, routes, router, w_gate, w_up, w_down):
@@ -529,10 +581,12 @@
     wide = -(-width // LANES) * LANES
     keys = ep_size * seq_dev
     group, group_slots = ep_size * tb // 2, ep_size * cap // 2
-    ufc = min(256, ff)
+    ufc = min(512, ff)
+    dfc = min(1024, model)
     fc = min(512, model)
-    down_steps = model // fc
-    dims = (zs, heads, width, latent, vdim, seq_dev, tb, model, ff, experts, cap, scale, ufc, fc)
+    send_steps = model // fc
+    dims = (zs, heads, width, latent, vdim, seq_dev, tb, model, ff, experts, cap, scale, ufc, dfc,
+            fc)
     cols = 2 * seq_dev
     vmem, dma = pltpu.VMEM, pltpu.SemaphoreType.DMA
     scratch = [
@@ -564,23 +618,23 @@
         vmem((zs - 1, tb, model), BF16),
         vmem((UP_SLOTS, model, ufc), BF16),
         vmem((UP_SLOTS, model, ufc), BF16),
-        vmem((DOWN_SLOTS, ff, fc), BF16),
+        vmem((DOWN_SLOTS, ff, dfc), BF16),
         dma((2, 2, 2)),
         dma((2, 2)),
         dma((2,)),
         dma((4 * zs - 1,)),
         dma((4 * zs,)),
-        dma((4 * zs - 1,)),
+        dma((5 * zs - 2,)),
         dma((4 * zs,)),
         dma((UP_SLOTS,)),
         dma((UP_SLOTS,)),
         dma((DOWN_SLOTS,)),
-        dma((down_steps,)),
-        dma((down_steps,)),
-        dma((down_steps,)),
-        dma((down_steps,)),
-        dma((down_steps, zs - 1)),
-        dma((down_steps, zs - 1)),
+        dma((send_steps,)),
+        dma((send_steps,)),
+        dma((send_steps,)),
+        dma((send_steps,)),
+        dma((send_steps, zs - 1)),
+        dma((send_steps, zs - 1)),
     ]
     hbm = pl.BlockSpec(memory_space=pl.ANY)
     local = pl.BlockSpec(memory_space=pltpu.VMEM)

time: 142 us -> 117 us (0.82)
  the two profiles are of different devices: /device:TPU:29 before, /device:TPU:0 now
where the time goes in v2:
time: 117 us
  Pallas kernels  111 us (95%)
  local copies, waits for them, and re-layouts  4.76 us (4%)
    pallas_call x1, Pallas kernels, per_device(): pl.pallas_call(functools.partial(layer_kernel, dims), in_specs=[hbm, hbm,...  111 us
    unnamed x2, local copies, waits for them, and re-layouts  4.76 us

profile of v2, /device:TPU:0, one launch (start us, length us, event | category | flops | bytes accessed | tf_op | source)
XLA Modules:
  0.0 116.6 jit_solution(49138407597668968)
XLA Ops:
  0.6 111.2 %shard_map.104 = (bf16[128,8192]{1,0:T(8,128)(2,1)}, bf16[32,4096]{1,0:T(8,128)(2,1)}) custom-call(bf16[64,576,128]{2,1,0:T(8,128)(2,1)} %bitcast.4, bf16[576,128]{1,0:T(8,128)(2,1)} %bitcast.5, bf16[64,512,128]{2,1,0:T(8,128)(2,1)} %wv_ref.1, bf16[32,4096]{1,0:T(8,128)(2,1)} %tok_ref.1, s32[8,32]{1,0:T(8,128)} %bitcast.7, bf16[16,4096]{1,0:T(8,128)(2,1)} %bitcast.6, ...), custom_call_target="tpu_custom_call" | custom-call | flops 36507222016 | bytes 50331648 | tf_op jit(solution)/shard_map/pallas_call | solution.py:641
  111.8 3.1 %copy.13 = bf16[128,8192]{1,0:T(8,128)(2,1)} copy(bf16[128,8192]{1,0:T(8,128)(2,1)} %get-tuple-element.4) | data formatting | bytes 4194304
  114.9 1.7 %copy.14 = bf16[32,4096]{1,0:T(8,128)(2,1)} copy(bf16[32,4096]{1,0:T(8,128)(2,1)} %get-tuple-element.5) | data formatting | bytes 524288

commit v3 on v2

--- a/solution.py
+++ b/solution.py
@@ -17,6 +17,7 @@
 UP_SLOTS = 2
 DOWN_SLOTS = 2
 MOE_AT = 7
+KV_PIECES = 2
 
 
 def layer_kernel(dims, q_ref, kv_ref, wv_ref, tok_ref, routes_ref, router_ref, wg_ref, wu_ref,
@@ -101,24 +102,25 @@
         pl.semaphore_signal(barrier, inc=1, device_id=peer, device_id_type=MESH)
     pl.semaphore_wait(barrier, zs + 1)
 
-    def kv_block(zz, xx, cc):
-        return kvt_all.at[
-            zz, pl.ds(0, width), pl.ds(pl.multiple_of((xx * 2 + cc) * seq_dev, seq_dev), seq_dev)
+    piece = width // KV_PIECES
+
+    def kv_send_to(zz, xx, cc, target, index, p):
+        block = kvt_all.at[
+            zz,
+            pl.ds(p * piece, piece),
+            pl.ds(pl.multiple_of((xx * 2 + cc) * seq_dev, seq_dev), seq_dev),
         ]
-
-    def kv_send_to(zz, xx, cc, target, index):
-        block = kv_block(zz, xx, cc)
         return pltpu.make_async_remote_copy(
             src_ref=block,
             dst_ref=block,
-            send_sem=kv_send.at[index],
-            recv_sem=kv_recv.at[zz * 4 + xx * 2 + cc],
+            send_sem=kv_send.at[index, p],
+            recv_sem=kv_recv.at[zz * 4 + xx * 2 + cc, p],
             device_id=target,
             device_id_type=MESH,
         )
 
-    def kv_wait(zz, xx, cc):
-        kv_send_to(zz, xx, cc, partner, 0).wait_recv()
+    def kv_wait(zz, xx, cc, p):
+        kv_send_to(zz, xx, cc, partner, 0, p).wait_recv()
 
     def kv_turn(zz, xx, cc):
         cols = pl.ds(pl.multiple_of((xx * 2 + cc) * seq_dev, seq_dev), seq_dev)
@@ -129,14 +131,15 @@
     for buf in (q_a, q_b):
         buf[:, width:, :] = jnp.zeros((2, buf.shape[1] - width, 2 * seq_dev), BF16)
     own_kv.wait()
-    def kv_up(d):
+    def kv_up(d, p):
         @pl.when(z + 1 < zs)
         def _():
-            kv_send_to(z - d, x, c, at(z + 1, x, c), d).start()
-
-    kv_up(0)
-    kv_send_to(z, x, c, across, zs - 1).start()
-    kv_send_to(z, x, c, partner, 2 * zs - 1).start()
+            kv_send_to(z - d, x, c, at(z + 1, x, c), d, p).start()
+
+    for p in range(KV_PIECES):
+        kv_up(0, p)
+        kv_send_to(z, x, c, across, zs - 1, p).start()
+        kv_send_to(z, x, c, partner, 2 * zs - 1, p).start()
 
     own_tok.wait()
 
@@ -181,11 +184,12 @@
 
         @pl.when(z - d >= 0)
         def _():
-            kv_wait(z - d, x, c)
-            if d < zs - 1:
-                kv_up(d)
-            kv_send_to(z - d, x, c, across, zs - 1 + d).start()
-            kv_send_to(z - d, x, c, partner, 2 * zs - 1 + d).start()
+            for p in range(KV_PIECES):
+                kv_wait(z - d, x, c, p)
+                if d < zs - 1:
+                    kv_up(d, p)
+                kv_send_to(z - d, x, c, across, zs - 1 + d, p).start()
+                kv_send_to(z - d, x, c, partner, 2 * zs - 1 + d, p).start()
             kv_turn(z - d, x, c)
 
     def tok_up(d):
@@ -216,8 +220,9 @@
 
         @pl.when(z - d >= 0)
         def _():
-            kv_wait(z - d, 1 - x, c)
-            kv_send_to(z - d, 1 - x, c, partner, 3 * zs - 1 + d).start()
+            for p in range(KV_PIECES):
+                kv_wait(z - d, 1 - x, c, p)
+                kv_send_to(z - d, 1 - x, c, partner, 3 * zs - 1 + d, p).start()
             kv_turn(z - d, 1 - x, c)
 
     for d in range(zs):
@@ -225,7 +230,8 @@
 
             @pl.when(z - d >= 0)
             def _():
-                kv_wait(z - d, xx, 1 - c)
+                for p in range(KV_PIECES):
+                    kv_wait(z - d, xx, 1 - c, p)
                 kv_turn(z - d, xx, 1 - c)
 
     def scores_of(n, q, s, diagonal):
@@ -537,7 +543,8 @@
 
         @pl.when((z + 1 < zs) & (z - d >= 0))
         def _():
-            kv_send_to(z, x, c, partner, d).wait_send()
+            for p in range(KV_PIECES):
+                kv_send_to(z, x, c, partner, d, p).wait_send()
 
         @pl.when((z + 1 < zs) & (z - d >= 0))
         def _():
@@ -552,7 +559,8 @@
         @pl.when(z - d >= 0)
         def _():
             for base in (zs - 1, 2 * zs - 1, 3 * zs - 1):
-                kv_send_to(z, x, c, partner, base + d).wait_send()
+                for p in range(KV_PIECES):
+                    kv_send_to(z, x, c, partner, base + d, p).wait_send()
 
     for index in range(3 * zs):
         tok_send_to(z, x, c, partner, index).wait_send()
@@ -622,8 +630,8 @@
         dma((2, 2, 2)),
         dma((2, 2)),
         dma((2,)),
-        dma((4 * zs - 1,)),
-        dma((4 * zs,)),
+        dma((4 * zs - 1, KV_PIECES)),
+        dma((4 * zs, KV_PIECES)),
         dma((5 * zs - 2,)),
         dma((4 * zs,)),
         dma((UP_SLOTS,)),

time: 117 us -> 115 us (0.983)
  Pallas kernels: 111 us -> 109 us
    pallas_call x1, Pallas kernels: 111 us -> 109 us  [per_device(): pl.pallas_call(functools.partial(layer_kernel, dims), in_specs=[hbm, hbm,...]
where the time goes in v3:
time: 115 us; the launch traced here: 114 us
  Pallas kernels  109 us (95%)
  local copies, waits for them, and re-layouts  4.76 us (4%)
    pallas_call x1, Pallas kernels, per_device(): pl.pallas_call(functools.partial(layer_kernel, dims), in_specs=[hbm, hbm,...  109 us
    unnamed x2, local copies, waits for them, and re-layouts  4.76 us

profile of v3, /device:TPU:0, one launch (start us, length us, event | category | flops | bytes accessed | tf_op | source)
XLA Modules:
  0.0 114.1 jit_solution(2978329228207268899)
XLA Ops:
  0.6 108.7 %shard_map.104 = (bf16[128,8192]{1,0:T(8,128)(2,1)}, bf16[32,4096]{1,0:T(8,128)(2,1)}) custom-call(bf16[64,576,128]{2,1,0:T(8,128)(2,1)} %bitcast.4, bf16[576,128]{1,0:T(8,128)(2,1)} %bitcast.5, bf16[64,512,128]{2,1,0:T(8,128)(2,1)} %wv_ref.1, bf16[32,4096]{1,0:T(8,128)(2,1)} %tok_ref.1, s32[8,32]{1,0:T(8,128)} %bitcast.7, bf16[16,4096]{1,0:T(8,128)(2,1)} %bitcast.6, ...), custom_call_target="tpu_custom_call" | custom-call | flops 36507222016 | bytes 50331648 | tf_op jit(solution)/shard_map/pallas_call | solution.py:649
  109.4 3.1 %copy.13 = bf16[128,8192]{1,0:T(8,128)(2,1)} copy(bf16[128,8192]{1,0:T(8,128)(2,1)} %get-tuple-element.4) | data formatting | bytes 4194304
  112.5 1.7 %copy.14 = bf16[32,4096]{1,0:T(8,128)(2,1)} copy(bf16[32,4096]{1,0:T(8,128)(2,1)} %get-tuple-element.5) | data formatting | bytes 524288
